TPU v7x, 32 devices: a whole 2x2x4 slice. The times are simulated.
32 devices in a mesh: tok: 16 (over z, y, core), tp: 2 (over x).
Axes of the slice: x: 2, y: 2, z: 4, core: 2. Of those that a mesh axis runs over, the one named last changes fastest.
Arguments:
- hidden: bfloat16 [1536, 8192], P('tok'), may hold values from -2600 to 2600
- norm_gain: float32 [8192], replicated, may hold values from 0.5 to 1.5
- w_query: bfloat16 [8192, 4096], P('tok', 'tp'), may hold values from -1 to 1
- w_key: bfloat16 [8192, 1024], P('tok', 'tp'), may hold values from -1 to 1
- w_value: bfloat16 [8192, 1024], P('tok', 'tp'), may hold values from -0.0625 to 0.0625
- doc_ids: int32 [1536], P('tok'), may hold values from 0 to 3, as said below
Outputs:
- attended: bfloat16 [1536, 4096], P('tok', 'tp')
- out_scale: float32 [4096], P('tp')
- folded_gain: float32 [8192], P(('tok', 'tp'))
- codes_query: float32 [8192, 4096], P(('tok', 'tp'))
- codes_key: float32 [8192, 1024], P(('tok', 'tp'))
- codes_value: float32 [8192, 1024], P(('tok', 'tp'))
- scale_query: float32 [4096], P('tp')
- scale_key: float32 [1024], P('tp')
- scale_value: float32 [1024], P('tp')
Inputs may be any that keep to these rules, and one draw needn't show every extreme that they name: doc_ids never falls along the tokens; each of the 4 documents holds 1 to 1152 tokens and one holds exactly 1152.
All inputs are finite; a program needn't handle non-finite values. Where the computation divides by a largest or mean magnitude, that divisor is 1e-20 or more.
Results may differ from a plain program's by a relative error of at most 0.005.
The roundings to bfloat16 on the way count: a program that leaves them out, or rounds other values in their place, can miss the bound.
Values may be sent and summed in bfloat16 or wider, within the bound.
A program may use at most 128 MiB of HBM per device.

v0:
```python
import math
import jax
import jax.numpy as jnp
from jax import lax
from jax.sharding import PartitionSpec as P

HEAD = 128
KVH = 8
QHEADS = 32


def rotate(states, positions):
    half = states.shape[-1] // 2
    inverse = jnp.exp(
        jnp.arange(half, dtype=jnp.float32) * (-2.0 * math.log(10000.0) / states.shape[-1])
    )
    angles = positions[:, None] * inverse[None, :]
    cosine = jnp.cos(angles)[:, None, :]
    sine = jnp.sin(angles)[:, None, :]
    first = states[..., :half]
    second = states[..., half:]
    return jnp.concatenate(
        [first * cosine - second * sine, second * cosine + first * sine], axis=-1
    )


def smooth_from(input_peak, weight_peak):
    return jnp.sqrt(jnp.maximum(input_peak, 1e-05)) / jnp.sqrt(jnp.maximum(weight_peak, 1e-05))


def head_to_rows(matrix, tp_index, tp_count):
    sub_rows = matrix.shape[0] // tp_count
    columns = matrix.shape[1]
    whole = jnp.zeros((sub_rows, columns * tp_count), matrix.dtype)
    for shift in range(tp_count):
        target = lax.rem(tp_index + shift, tp_count)
        source = lax.rem(tp_index - shift + tp_count, tp_count)
        block = lax.dynamic_slice_in_dim(matrix, target * sub_rows, sub_rows)
        if shift > 0:
            pairs = [(i, (i + shift) % tp_count) for i in range(tp_count)]
            block = lax.ppermute(block, "tp", pairs)
        whole = lax.dynamic_update_slice_in_dim(whole, block, source * columns, axis=1)
    return whole


def on_device(hidden, norm_gain, w_query, w_key, w_value, doc_ids):
    tok_dev = hidden.shape[0]
    row_count = w_query.shape[0]
    tp_count = lax.axis_size("tp")
    tok_index = lax.axis_index("tok")
    tp_index = lax.axis_index("tp")
    heads_here = w_query.shape[1] // HEAD
    kv_here = w_key.shape[1] // HEAD
    group_size = QHEADS // KVH
    matrices = (w_query, w_key, w_value)
    states = hidden.astype(jnp.float32)
    normed = (
        states
        * lax.rsqrt(jnp.mean(states * states, axis=1, keepdims=True) + 1e-05)
        * norm_gain[None, :]
    ).astype(jnp.bfloat16)
    token_side = lax.all_to_all(normed, "tok", split_axis=1, concat_axis=0, tiled=True)
    input_rows = jnp.max(jnp.abs(token_side), axis=0).astype(jnp.float32)
    relaid = tuple((head_to_rows(matrix, tp_index, tp_count) for matrix in matrices))
    partial = jnp.dot(
        token_side, jnp.concatenate(matrices, axis=1), preferred_element_type=jnp.float32
    )
    summed = lax.psum_scatter(partial, "tok", scatter_dimension=0, tiled=True)
    query_columns, key_columns = (w_query.shape[1], w_key.shape[1])
    projected = (
        summed[:, :query_columns],
        summed[:, query_columns : query_columns + key_columns],
        summed[:, query_columns + key_columns :],
    )
    local_peak = jnp.max(
        jnp.stack([jnp.max(jnp.abs(matrix), axis=1) for matrix in matrices]), axis=0
    ).astype(jnp.float32)
    row_peak = lax.pmax(local_peak, "tp")
    smoothing_rows = smooth_from(input_rows, row_peak)
    column_local = tuple(
        (
            jnp.max(jnp.abs(smoothing_rows[:, None] * matrix.astype(jnp.float32)), axis=0)
            for matrix in matrices
        )
    )
    column_global = lax.pmax(column_local, "tok")
    scales = tuple((jnp.maximum(column, 1e-05) / 127.0 for column in column_global))
    query_positions = tok_index * tok_dev + jnp.arange(tok_dev, dtype=jnp.int32)
    positions = query_positions.astype(jnp.float32)
    query = (
        rotate(projected[0].reshape(tok_dev, heads_here, HEAD), positions)
        .astype(jnp.bfloat16)
        .reshape(tok_dev, kv_here, group_size, HEAD)
    )
    key = (
        rotate(projected[1].reshape(tok_dev, kv_here, HEAD), positions)
        .astype(jnp.bfloat16)
        .reshape(tok_dev, kv_here * HEAD)
    )
    value = projected[2].astype(jnp.bfloat16)
    score_scale = 1.0 / math.sqrt(HEAD)
    highest = jnp.full((kv_here, group_size, tok_dev), -1e30, jnp.float32)
    key_block = lax.all_gather(key, "tok", axis=0, tiled=True)
    value_block = lax.all_gather(value, "tok", axis=0, tiled=True)
    doc_block = lax.all_gather(doc_ids, "tok", axis=0, tiled=True)
    length = key_block.shape[0]
    scores = (
        jnp.einsum(
            "tkgd,skd->kgts",
            query,
            key_block.reshape(length, kv_here, HEAD),
            preferred_element_type=jnp.float32,
        )
        * score_scale
    )
    key_positions = jnp.arange(length, dtype=jnp.int32)
    allowed = (doc_ids[:, None] == doc_block[None, :]) & (
        key_positions[None, :] <= query_positions[:, None]
    )
    scores = jnp.where(allowed, scores, -1e30)
    raised = jnp.maximum(highest, jnp.max(scores, axis=3))
    weights = jnp.where(allowed, jnp.exp(scores - raised[..., None]), 0.0)
    totals = jnp.sum(weights, axis=3)
    accumulated = jnp.einsum(
        "kgts,skd->kgtd",
        weights.astype(jnp.bfloat16),
        value_block.reshape(length, kv_here, HEAD),
        preferred_element_type=jnp.float32,
    )
    highest, totals, accumulated = (raised, totals, accumulated)
    attended = (
        (accumulated / totals[..., None])
        .transpose(2, 0, 1, 3)
        .reshape(tok_dev, heads_here * HEAD)
        .astype(jnp.bfloat16)
    )
    out_scale = lax.pmax(jnp.max(jnp.abs(attended), axis=0).astype(jnp.float32), "tok")
    sub_rows = row_count // tp_count
    smooth_part = lax.dynamic_slice_in_dim(smoothing_rows, tp_index * sub_rows, sub_rows)
    gain_part = lax.dynamic_slice_in_dim(
        norm_gain, tok_index * row_count + tp_index * sub_rows, sub_rows
    )
    folded_gain = gain_part / smooth_part
    every_scale = lax.all_gather(scales, "tp", axis=0, tiled=True)
    codes = tuple(
        (
            smooth_part[:, None] * block.astype(jnp.float32) / column_scale[None, :]
            for block, column_scale in zip(relaid, every_scale)
        )
    )
    return (
        attended,
        out_scale,
        folded_gain,
        codes[0],
        codes[1],
        codes[2],
        scales[0],
        scales[1],
        scales[2],
    )


def solution(mesh):
    in_specs = (P("tok", None), P(), P("tok", "tp"), P("tok", "tp"), P("tok", "tp"), P("tok"))
    out_specs = (
        P("tok", "tp"),
        P("tp"),
        P(("tok", "tp")),
        P(("tok", "tp"), None),
        P(("tok", "tp"), None),
        P(("tok", "tp"), None),
        P("tp"),
        P("tp"),
        P("tp"),
    )
    return jax.shard_map(
        on_device, mesh=mesh, in_specs=in_specs, out_specs=out_specs, check_vma=False
    )
```

profile of v0, /device:TPU:0, one launch (start us, length us, event | category | flops | bytes accessed | tf_op | source)
XLA Modules:
  0.0 442.9 jit_solution(13857068211997247535)
XLA Ops:
  7.2 0.0 reduce-scatter.2.cloned.1.call-start
  7.2 1.8 fusion.6
  9.1 1.9 fusion.8
  11.0 0.1 copy.59
  11.1 43.3 %all_to_all.19 = bf16[96,16,512]{2,0,1:T(8,128)(2,1)S(1)} all-to-all(bf16[96,16,512]{2,0,1:T(8,128)(2,1)S(1)} %bitcast.63), channel_id=1, replica_groups=mesh['tok'=16,'tp'=2] {'tok'}, dimensions={1} | all-to-all | bytes 3145728 | tf_op jit(solution)/shard_map/all_to_all | solution.py:62
  54.4 1.1 copy-done.2
  55.5 9.2 %fusion.9 = f32[1536,3072]{1,0:T(8,128)} fusion(bf16[1536,512]{1,0:T(8,128)(2,1)S(1)} %bitcast.62, bf16[512,512]{1,0:T(8,128)(2,1)S(1)} %copy-done.3, bf16[512,512]{1,0:T(8,128)(2,1)S(1)} %copy-done.4, bf16[512,2048]{1,0:T(8,128)(2,1)S(1)} %copy-done.1), kind=kOutput, calls=%fused_computation.14 | convolution fusion | flops 4841275392 | bytes 23592960 | tf_op jit(solution)/shard_map/dot_general | solution.py:65
  64.8 0.0 reduce-scatter.2.cloned.1.call-update
  64.8 0.0 all-gather.5.cloned.1.call-start
  64.9 0.9 multiply_cosine_fusion
  65.8 193.7 %reduce-scatter.2.cloned.1.call-done = f32[96,3072]{1,0:T(8,128)} async-done(((f32[1536,3072]{1,0:T(8,128)}), f32[96,3072]{1,0:T(8,128)}) %reduce-scatter.2.cloned.1.call-update) | async-done | bytes 1179664 | tf_op jit(solution)/shard_map/reduce_scatter | solution.py:68
  259.4 0.9 slice.29
  260.4 0.1 reshape.128
  260.4 1.0 subtract_convert_fusion.1
  261.5 0.1 pad_maximum_fusion
  261.6 0.7 copy.60
  262.3 0.0 all-gather.7.cloned.1.call-start
  262.4 0.9 broadcast.88.clone
  263.3 0.8 constant_dynamic-slice_fusion.1
  264.1 1.4 collective-permute-start.2
  265.5 0.8 broadcast.88.clone.1
  266.3 0.9 constant_dynamic-slice_fusion
  267.2 0.6 collective-permute-start.1
  267.8 1.6 broadcast_in_dim.18
  269.3 1.5 constant_dynamic-slice_fusion.2
  270.9 1.5 collective-permute-start
  272.4 0.6 dynamic-slice
  273.6 0.3 dynamic-update-slice
  273.9 10.8 %all-reduce = s32[1536]{0:T(1024)} all-reduce(s32[1536]{0:T(1024)S(1)} %dynamic-update-slice), channel_id=1, replica_groups=mesh['tok'=16,'tp'=2] {'tok'}, use_global_device_ids=true, to_apply=%add | all-reduce | flops 1536 | bytes 12288
  284.8 0.7 abs_reduce_fusion.4
  285.5 1.0 abs_reduce_fusion.1
  286.5 0.9 fusion.32
  287.5 0.7 abs_reduce_fusion.5
  288.2 1.3 maximum_convert_fusion
  289.5 11.3 %pmax.36 = f32[512]{0:T(512)} all-reduce(f32[512]{0:T(512)} %maximum_convert_fusion), channel_id=1, replica_groups=mesh['tok'=16,'tp'=2] {'tp'}, use_global_device_ids=true, to_apply=%region_10.0 | all-reduce | flops 512 | bytes 4096 | tf_op jit(solution)/shard_map/pmax | solution.py:78
  300.8 1.7 constant_dynamic-update-slice_fusion
  302.5 1.7 constant_dynamic-update-slice_fusion.1
  304.2 2.3 constant_dynamic-update-slice_fusion.2
  306.5 1.6 slice.46
  308.1 1.7 fusion.16
  309.8 1.3 dynamic-slice_divide_fusion
  311.2 0.3 abs_reduce_fusion.2
  311.5 0.5 abs_reduce_fusion
  312.0 0.1 slice_bitcast_fusion
  312.1 0.1 copy.46
  312.3 0.4 subtract_convert_fusion
  312.7 0.1 copy.33
  312.8 0.1 copy.34
  312.9 0.0 all-gather.5.cloned.1.call-done
  312.9 1.7 copy.32
  314.6 2.0 fusion
  316.6 3.6 copy-done
  320.2 2.8 fusion.1
  323.0 24.2 %all-gather.7.cloned.1.call-done = bf16[1536,512]{1,0:T(8,128)(2,1)} async-done(((bf16[96,512]{1,0:T(8,128)(2,1)}), bf16[1536,512]{1,0:T(8,128)(2,1)}) %all-gather.7.cloned.1.call-update) | async-done | bytes 1572880 | tf_op jit(solution)/shard_map/all_gather | solution.py:104
  347.2 2.4 reshape.131
  349.6 6.0 %abs_reduce_fusion.6 = (bf16[4,4,128]{2,1,0:T(4,128)(2,1)S(1)}, bf16[96,4,4,128]{3,0,2,1:T(8,128)(2,1)S(1)}) fusion(f32[96,4,4]{0,2,1:T(4,128)S(1)} %bitcast.72, bf16[1536,4,128,1]{2,1,0,3:T(4,128)(2,1)S(1)} %bitcast.65, f32[4,1536,96,4]{1,2,3,0:T(8,128)} %copy-done, f32[4,4,96]{2,1,0:T(4,128)S(1)} %broadcast_maximum_fusion, pred[96,1536]{1,0:T(8,128)(4,1)S(1)} %fusion.32), kind=kOutput, calls=%fused_computation.44 | convolution fusion | flops 616560640 | bytes 11567104 | tf_op jit(solution)/shard_map/kgts,skd->kgtd/dot_general | solution.py:124
  355.6 59.4 %all-reduce.1 = (f32[2048]{0:T(1024)}, f32[2048]{0:T(1024)S(1)}, f32[512]{0:T(512)S(1)}, f32[512]{0:T(512)S(1)}) all-reduce(bf16[2048]{0:T(1024)(128)(2,1)S(1)} %bitcast.75, f32[2048]{0:T(1024)S(1)} %abs_reduce_fusion, f32[512]{0:T(512)S(1)} %get-tuple-element.10, f32[512]{0:T(512)S(1)} %get-tuple-element.9), channel_id=1, replica_groups=mesh['tok'=16,'tp'=2] {'tok'}, use_global_device_ids=true, to_apply=%region_5.0 | all-reduce | flops 5120 | bytes 36864 | tf_op jit(solution)/shard_map/pmax | solution.py:137
  415.0 4.4 all-gather
  419.3 4.4 all-gather.1
  423.7 4.4 all_gather.21
  428.1 0.2 copy.37
  428.3 1.0 convert_element_type.67
  429.3 4.3 multiply_divide_fusion
  433.6 2.8 multiply_divide_fusion.1
  (41 shorter events, 0.2 us)
Async XLA Ops:
  7.2 252.2 %reduce-scatter.2.cloned.1.call-start = ((), (), s32[]{:S(2)}) async-start(), calls=%async_computation.2 | async-start | bytes 20054016 | tf_op jit(solution)/shard_map/reduce_scatter | solution.py:68
  10.9 44.6 %copy-start.1 = (bf16[512,2048]{1,0:T(8,128)(2,1)S(1)}, bf16[512,2048]{1,0:T(8,128)(2,1)}, u32[]{:S(2)}) copy-start(bf16[512,2048]{1,0:T(8,128)(2,1)} %param.8) | copy-start | bytes 6291460
  10.9 44.6 %copy-start.3 = (bf16[512,512]{1,0:T(8,128)(2,1)S(1)}, bf16[512,512]{1,0:T(8,128)(2,1)}, u32[]{:S(2)}) copy-start(bf16[512,512]{1,0:T(8,128)(2,1)} %param.10) | copy-start | bytes 1572868
  11.0 44.6 %copy-start.4 = (bf16[512,512]{1,0:T(8,128)(2,1)S(1)}, bf16[512,512]{1,0:T(8,128)(2,1)}, u32[]{:S(2)}) copy-start(bf16[512,512]{1,0:T(8,128)(2,1)} %param.9) | copy-start | bytes 1572868
  54.4 1.1 copy-start.2
  64.8 248.1 %all-gather.5.cloned.1.call-start = ((), (), s32[]{:S(2)}) async-start(), calls=%async_computation.3 | async-start | bytes 1671168 | tf_op jit(solution)/shard_map/all_gather | solution.py:103
  262.3 85.0 %all-gather.7.cloned.1.call-start = ((), (), s32[]{:S(2)}) async-start(), calls=%async_computation.4 | async-start | bytes 1671168 | tf_op jit(solution)/shard_map/all_gather | solution.py:104
  264.1 36.7 %collective-permute-start.2 = (bf16[256,512]{1,0:T(8,128)(2,1)S(1)}, bf16[256,512]{1,0:T(8,128)(2,1)}, u32[]{:S(2)}, u32[]{:S(2)}) collective-permute-start(bf16[256,512]{1,0:T(8,128)(2,1)S(1)} %get-tuple-element.21), channel_id=1, source_target_pairs={{0,1},{1,0},{2,3},{3,2},{4,5},{5,4},{6,7},{7,6},{8,9},{9,8},{10,11... | collective-permute-start | bytes 786440 | tf_op jit(solution)/shard_map/ppermute | solution.py:41
  267.2 35.3 %collective-permute-start.1 = (bf16[256,512]{1,0:T(8,128)(2,1)}, bf16[256,512]{1,0:T(8,128)(2,1)}, u32[]{:S(2)}, u32[]{:S(2)}) collective-permute-start(bf16[256,512]{1,0:T(8,128)(2,1)} %get-tuple-element.23), channel_id=1, source_target_pairs={{0,1},{1,0},{2,3},{3,2},{4,5},{5,4},{6,7},{7,6},{8,9},{9,8},{10,11... | collective-permute-start | bytes 786440 | tf_op jit(solution)/shard_map/ppermute | solution.py:41
  267.8 4.6 %copy-start.13 = (u32[32]{0:T(128)S(1)}, u32[32]{0:T(128)}, u32[]{:S(2)}) copy-start(u32[32]{0:T(128)} %constant.69) | copy-start | bytes 388
  267.8 5.9 %copy-start.12 = (s32[96]{0:T(128)S(1)}, s32[96]{0:T(128)}, u32[]{:S(2)}) copy-start(s32[96]{0:T(128)} %param.11) | copy-start | bytes 1156
  270.9 33.3 %collective-permute-start = (bf16[256,2048]{1,0:T(8,128)(2,1)}, bf16[256,2048]{1,0:T(8,128)(2,1)}, u32[]{:S(2)}, u32[]{:S(2)}) collective-permute-start(bf16[256,2048]{1,0:T(8,128)(2,1)} %get-tuple-element.17), channel_id=1, source_target_pairs={{0,1},{1,0},{2,3},{3,2},{4,5},{5,4},{6,7},{7,6},{8,9},{9,8},{10,11... | collective-permute-start | bytes 3145736 | tf_op jit(solution)/shard_map/ppermute | solution.py:41
  300.8 9.0 %copy-start.11 = (f32[512]{0:T(512)S(1)}, f32[512]{0:T(512)}, u32[]{:S(2)}) copy-start(f32[512]{0:T(512)} %pmax.36) | copy-start | bytes 6148
  308.1 3.9 copy-start.5
  311.2 1.1 copy-start.6
  311.2 1.1 copy-start.7
  316.6 3.6 copy-start
  415.0 18.6 %copy-start.9 = (f32[512]{0:T(512)}, f32[512]{0:T(512)S(1)}, u32[]{:S(2)}) copy-start(f32[512]{0:T(512)S(1)} %maximum_multiply_fusion.2) | copy-start | bytes 6148
  419.3 14.3 %copy-start.10 = (f32[512]{0:T(512)}, f32[512]{0:T(512)S(1)}, u32[]{:S(2)}) copy-start(f32[512]{0:T(512)S(1)} %maximum_multiply_fusion.1) | copy-start | bytes 6148
  423.7 9.9 %copy-start.8 = (f32[2048]{0:T(1024)}, f32[2048]{0:T(1024)S(1)}, u32[]{:S(2)}) copy-start(f32[2048]{0:T(1024)S(1)} %maximum_multiply_fusion) | copy-start | bytes 24580
Sparse Core Ops, SparseCore 0:
  64.9 194.4 reduce-scatter.1
  262.4 38.6 all-gather.4
  308.3 38.9 all-gather.6
where the time goes:
time: 444 us; the launch traced here: 443 us
  waiting for transfers between devices  218 us (49%)
  blocking collectives  138 us (31%)
  local copies, waits for them, and re-layouts  27 us (6%)
  other arithmetic  24.6 us (6%)
  matrix products  17.2 us (4%)
  between operations  14.7 us (3%)
    reduce_scatter x1, waiting for transfers between devices, on_device(): summed = lax.psum_scatter(partial, 'tok', scatter_dimension=0, tiled=True)  194 us
    pmax x1, blocking collectives, on_device(): lax.pmax(jnp.max(jnp.abs(attended), axis=0).astype(jnp.float32), 'tok')  59.4 us
    all_to_all x1, blocking collectives, on_device(): lax.all_to_all(normed, 'tok', split_axis=1, concat_axis=0, tiled=True)  43.3 us
    all_gather x1, waiting for transfers between devices, on_device(): value_block = lax.all_gather(value, 'tok', axis=0, tiled=True)  24.2 us
    all_gather x3, blocking collectives, on_device(): every_scale = lax.all_gather(scales, 'tp', axis=0, tiled=True)  13.1 us
    pmax x1, blocking collectives, on_device(): row_peak = lax.pmax(local_peak, 'tp')  11.3 us
    unnamed x1, blocking collectives  10.8 us
    dot_general x1, matrix products, on_device(): jnp.dot(token_side, jnp.concatenate(matrices, axis=1), preferred_element_...  9.24 us
  transfers between devices with their start and end apart: 6, of which 2 were waited for; matrix products, arithmetic and copies ran while one was open for 7% of the time, Pallas kernels for 0%

commit v1 on v0

--- a/solution.py
+++ b/solution.py
@@ -101,7 +101,13 @@
     score_scale = 1.0 / math.sqrt(HEAD)
     highest = jnp.full((kv_here, group_size, tok_dev), -1e30, jnp.float32)
     key_block = lax.all_gather(key, "tok", axis=0, tiled=True)
-    value_block = lax.all_gather(value, "tok", axis=0, tiled=True)
+    n_dev = lax.axis_size("tok")
+    moving, shards = (value, [value])
+    for _ in range(n_dev - 1):
+        moving = lax.ppermute(moving, "tok", [(i_2, (i_2 + 1) % n_dev) for i_2 in range(n_dev)])
+        shards.insert(0, moving)
+    row_of_blocks = jnp.concatenate(shards, axis=0)
+    value_block = jnp.roll(row_of_blocks, (lax.axis_index("tok") + 1) * value.shape[0], axis=0)
     doc_block = lax.all_gather(doc_ids, "tok", axis=0, tiled=True)
     length = key_block.shape[0]
     scores = (

time: 444 us -> 482 us (1.086)
  waiting for transfers between devices: 218 us -> 270 us
  blocking collectives: 138 us -> 132 us
    ppermute x0 -> x15, waiting for transfers between devices: none -> 80.8 us  [on_device(): lax.ppermute(moving, 'tok', [(i_2, (i_2 + 1) % n_dev) for i_2 in range(n_...]
    all_gather x1 -> x0, waiting for transfers between devices: 24.2 us -> none  [on_device(): value_block = lax.all_gather(value, 'tok', axis=0, tiled=True)]
    reduce_scatter x1, waiting for transfers between devices: 194 us -> 170 us  [on_device(): summed = lax.psum_scatter(partial, 'tok', scatter_dimension=0, tiled=True)]
    all_gather x1, waiting for transfers between devices: 0.02 us -> 19.6 us  [on_device(): key_block = lax.all_gather(key, 'tok', axis=0, tiled=True)]
    pmax x1, blocking collectives: 11.3 us -> 4.93 us  [on_device(): row_peak = lax.pmax(local_peak, 'tp')]
  transfers between devices with their start and end apart: 6 -> 20, of which waited for: 2 -> 17; matrix products, arithmetic and copies ran while one was open for 7% -> 5% of each run, Pallas kernels for 0% -> 0%
where the time goes in v1:
time: 482 us
  waiting for transfers between devices  270 us (56%)
  blocking collectives  132 us (27%)
  local copies, waits for them, and re-layouts  25.1 us (5%)
  other arithmetic  20 us (4%)
  between operations  15.5 us (3%)
  matrix products  14.9 us (3%)
    reduce_scatter x1, waiting for transfers between devices, on_device(): summed = lax.psum_scatter(partial, 'tok', scatter_dimension=0, tiled=True)  170 us
    ppermute x15, waiting for transfers between devices, on_device(): lax.ppermute(moving, 'tok', [(i_2, (i_2 + 1) % n_dev) for i_2 in range(n_...  80.8 us
    pmax x1, blocking collectives, on_device(): lax.pmax(jnp.max(jnp.abs(attended), axis=0).astype(jnp.float32), 'tok')  59.4 us
    all_to_all x1, blocking collectives, on_device(): lax.all_to_all(normed, 'tok', split_axis=1, concat_axis=0, tiled=True)  43.3 us
    all_gather x1, waiting for transfers between devices, on_device(): key_block = lax.all_gather(key, 'tok', axis=0, tiled=True)  19.6 us
    all_gather x3, blocking collectives, on_device(): every_scale = lax.all_gather(scales, 'tp', axis=0, tiled=True)  13.1 us
    unnamed x1, blocking collectives  11.6 us
  transfers between devices with their start and end apart: 20, of which 17 were waited for; matrix products, arithmetic and copies ran while one was open for 5% of the time, Pallas kernels for 0%

profile of v1, /device:TPU:0, one launch (start us, length us, event | category | flops | bytes accessed | tf_op | source)
XLA Modules:
  0.0 481.5 jit_solution(5598340029187787315)
XLA Ops:
  7.2 1.8 fusion.6
  9.1 1.9 fusion.8
  11.1 43.3 %all_to_all.19 = bf16[96,16,512]{2,0,1:T(8,128)(2,1)S(1)} all-to-all(bf16[96,16,512]{2,0,1:T(8,128)(2,1)S(1)} %bitcast.68), channel_id=1, replica_groups=mesh['tok'=16,'tp'=2] {'tok'}, dimensions={1} | all-to-all | bytes 3145728 | tf_op jit(solution)/shard_map/all_to_all | solution.py:62
  54.4 1.1 copy-done.1
  55.5 9.2 %fusion.9 = f32[1536,3072]{1,0:T(8,128)} fusion(bf16[1536,512]{1,0:T(8,128)(2,1)S(1)} %bitcast.67, bf16[512,512]{1,0:T(8,128)(2,1)S(1)} %copy-done.3, bf16[512,512]{1,0:T(8,128)(2,1)S(1)} %copy-done.4, bf16[512,2048]{1,0:T(8,128)(2,1)S(1)} %copy-done), kind=kOutput, calls=%fused_computation.14 | convolution fusion | flops 4841275392 | bytes 23592960 | tf_op jit(solution)/shard_map/dot_general | solution.py:65
  64.8 0.9 broadcast.88.clone
  65.7 0.8 constant_dynamic-slice_fusion.1
  66.6 1.5 collective-permute-start.17
  68.0 0.8 broadcast.88.clone.1
  68.9 0.8 constant_dynamic-slice_fusion
  69.7 0.5 collective-permute-start.16
  70.3 1.5 broadcast_in_dim.18
  71.8 1.6 constant_dynamic-slice_fusion.2
  73.5 1.5 collective-permute-start.15
  75.0 0.6 dynamic-slice
  76.5 11.6 %all-reduce = s32[1536]{0:T(1024)S(1)} all-reduce(s32[1536]{0:T(1024)S(1)} %dynamic-update-slice), channel_id=1, replica_groups=mesh['tok'=16,'tp'=2] {'tok'}, use_global_device_ids=true, to_apply=%add | all-reduce | flops 1536 | bytes 12288
  88.4 0.9 multiply_cosine_fusion
  89.2 0.5 abs_reduce_fusion.1
  89.7 169.7 %reduce-scatter.2.cloned.1.call-done = f32[96,3072]{1,0:T(8,128)} async-done(((f32[1536,3072]{1,0:T(8,128)}), f32[96,3072]{1,0:T(8,128)}) %reduce-scatter.2.cloned.1.call-update) | async-done | bytes 1179664 | tf_op jit(solution)/shard_map/reduce_scatter | solution.py:68
  259.4 0.9 slice.46
  260.6 6.5 %collective-permute-done = bf16[96,512]{1,0:T(8,128)(2,1)S(1)} collective-permute-done((bf16[96,512]{1,0:T(8,128)(2,1)S(1)}, bf16[96,512]{1,0:T(8,128)(2,1)S(1)}, u32[]{:S(2)}, u32[]{:S(2)}) %collective-permute-start) | collective-permute-done | bytes 98336 | tf_op jit(solution)/shard_map/ppermute | solution.py:107
  267.1 0.6 copy-done.7
  267.9 6.6 %collective-permute-done.1 = bf16[96,512]{1,0:T(8,128)(2,1)S(1)} collective-permute-done((bf16[96,512]{1,0:T(8,128)(2,1)S(1)}, bf16[96,512]{1,0:T(8,128)(2,1)S(1)}, u32[]{:S(2)}, u32[]{:S(2)}) %collective-permute-start.1) | collective-permute-done | bytes 98336 | tf_op jit(solution)/shard_map/ppermute | solution.py:107
  274.5 4.9 %pmax.36 = f32[512]{0:T(512)S(1)} all-reduce(f32[512]{0:T(512)S(1)} %maximum_convert_fusion), channel_id=1, replica_groups=mesh['tok'=16,'tp'=2] {'tp'}, use_global_device_ids=true, to_apply=%region_10.0 | all-reduce | flops 512 | bytes 4096 | tf_op jit(solution)/shard_map/pmax | solution.py:78
  279.5 1.8 collective-permute-done.2
  281.2 1.7 constant_dynamic-update-slice_fusion.32
  283.0 5.0 %collective-permute-done.3 = bf16[96,512]{1,0:T(8,128)(2,1)S(1)} collective-permute-done((bf16[96,512]{1,0:T(8,128)(2,1)S(1)}, bf16[96,512]{1,0:T(8,128)(2,1)S(1)}, u32[]{:S(2)}, u32[]{:S(2)}) %collective-permute-start.3) | collective-permute-done | bytes 98336 | tf_op jit(solution)/shard_map/ppermute | solution.py:107
  288.0 1.7 constant_dynamic-update-slice_fusion.33
  289.7 5.0 %collective-permute-done.4 = bf16[96,512]{1,0:T(8,128)(2,1)S(1)} collective-permute-done((bf16[96,512]{1,0:T(8,128)(2,1)S(1)}, bf16[96,512]{1,0:T(8,128)(2,1)S(1)}, u32[]{:S(2)}, u32[]{:S(2)}) %collective-permute-start.4) | collective-permute-done | bytes 98336 | tf_op jit(solution)/shard_map/ppermute | solution.py:107
  294.8 2.4 constant_dynamic-update-slice_fusion.34
  297.2 4.2 collective-permute-done.5
  301.6 6.5 %collective-permute-done.6 = bf16[96,512]{1,0:T(8,128)(2,1)S(1)} collective-permute-done((bf16[96,512]{1,0:T(8,128)(2,1)S(1)}, bf16[96,512]{1,0:T(8,128)(2,1)S(1)}, u32[]{:S(2)}, u32[]{:S(2)}) %collective-permute-start.6) | collective-permute-done | bytes 98336 | tf_op jit(solution)/shard_map/ppermute | solution.py:107
  308.2 0.6 copy-done.19
  308.8 6.1 %collective-permute-done.7 = bf16[96,512]{1,0:T(8,128)(2,1)S(1)} collective-permute-done((bf16[96,512]{1,0:T(8,128)(2,1)S(1)}, bf16[96,512]{1,0:T(8,128)(2,1)S(1)}, u32[]{:S(2)}, u32[]{:S(2)}) %collective-permute-start.7) | collective-permute-done | bytes 98336 | tf_op jit(solution)/shard_map/ppermute | solution.py:107
  314.9 0.5 abs_reduce_fusion
  315.5 6.2 %collective-permute-done.8 = bf16[96,512]{1,0:T(8,128)(2,1)S(1)} collective-permute-done((bf16[96,512]{1,0:T(8,128)(2,1)S(1)}, bf16[96,512]{1,0:T(8,128)(2,1)S(1)}, u32[]{:S(2)}, u32[]{:S(2)}) %collective-permute-start.8) | collective-permute-done | bytes 98336 | tf_op jit(solution)/shard_map/ppermute | solution.py:107
  321.7 0.9 abs_reduce_fusion.2
  322.6 5.9 %collective-permute-done.9 = bf16[96,512]{1,0:T(8,128)(2,1)S(1)} collective-permute-done((bf16[96,512]{1,0:T(8,128)(2,1)S(1)}, bf16[96,512]{1,0:T(8,128)(2,1)S(1)}, u32[]{:S(2)}, u32[]{:S(2)}) %collective-permute-start.9) | collective-permute-done | bytes 98336 | tf_op jit(solution)/shard_map/ppermute | solution.py:107
  328.4 1.4 dynamic-slice_divide_fusion
  329.9 5.3 %collective-permute-done.10 = bf16[96,512]{1,0:T(8,128)(2,1)S(1)} collective-permute-done((bf16[96,512]{1,0:T(8,128)(2,1)S(1)}, bf16[96,512]{1,0:T(8,128)(2,1)S(1)}, u32[]{:S(2)}, u32[]{:S(2)}) %collective-permute-start.10) | collective-permute-done | bytes 98336 | tf_op jit(solution)/shard_map/ppermute | solution.py:107
  335.2 1.0 subtract_convert_fusion.1
  336.2 5.7 %collective-permute-done.11 = bf16[96,512]{1,0:T(8,128)(2,1)S(1)} collective-permute-done((bf16[96,512]{1,0:T(8,128)(2,1)S(1)}, bf16[96,512]{1,0:T(8,128)(2,1)S(1)}, u32[]{:S(2)}, u32[]{:S(2)}) %collective-permute-start.11) | collective-permute-done | bytes 98336 | tf_op jit(solution)/shard_map/ppermute | solution.py:107
  342.0 0.7 copy.52
  342.7 5.9 %collective-permute-done.12 = bf16[96,512]{1,0:T(8,128)(2,1)S(1)} collective-permute-done((bf16[96,512]{1,0:T(8,128)(2,1)S(1)}, bf16[96,512]{1,0:T(8,128)(2,1)S(1)}, u32[]{:S(2)}, u32[]{:S(2)}) %collective-permute-start.12) | collective-permute-done | bytes 98336 | tf_op jit(solution)/shard_map/ppermute | solution.py:107
  348.6 1.2 slice_bitcast_fusion
  350.0 5.4 %collective-permute-done.13 = bf16[96,512]{1,0:T(8,128)(2,1)S(1)} collective-permute-done((bf16[96,512]{1,0:T(8,128)(2,1)S(1)}, bf16[96,512]{1,0:T(8,128)(2,1)S(1)}, u32[]{:S(2)}, u32[]{:S(2)}) %collective-permute-start.13) | collective-permute-done | bytes 98336 | tf_op jit(solution)/shard_map/ppermute | solution.py:107
  355.6 0.4 subtract_convert_fusion
  355.9 0.8 copy.34
  356.8 0.8 copy.35
  357.6 4.6 collective-permute-done.14
  362.9 0.4 constant_dynamic-slice_fusion.3
  363.3 0.7 copy.37
  364.0 19.6 %all-gather.4.cloned.1.call-done = bf16[1536,512]{1,0:T(8,128)(2,1)} async-done(((bf16[96,512]{1,0:T(8,128)(2,1)}), bf16[1536,512]{1,0:T(8,128)(2,1)}) %all-gather.4.cloned.1.call-update) | async-done | bytes 1572880 | tf_op jit(solution)/shard_map/all_gather | solution.py:103
  383.6 1.7 copy.33
  385.3 3.1 fusion
  388.5 2.8 fusion.1
  391.3 2.6 abs_reduce_fusion.6
  393.9 59.4 %all-reduce.1 = (f32[2048]{0:T(1024)}, f32[2048]{0:T(1024)S(1)}, f32[512]{0:T(512)S(1)}, f32[512]{0:T(512)S(1)}) all-reduce(bf16[2048]{0:T(1024)(128)(2,1)S(1)} %bitcast.80, f32[2048]{0:T(1024)S(1)} %abs_reduce_fusion, f32[512]{0:T(512)S(1)} %copy-done.30, f32[512]{0:T(512)S(1)} %get-tuple-element.9), channel_id=1, replica_groups=mesh['tok'=16,'tp'=2] {'tok'}, use_global_device_ids=true, to_apply=%region_5.0 | all-reduce | flops 5120 | bytes 36864 | tf_op jit(solution)/shard_map/pmax | solution.py:143
  453.3 4.4 all-gather
  457.6 4.4 all-gather.1
  462.0 4.4 all_gather.17
  466.6 1.0 convert_element_type.67
  467.6 4.3 multiply_divide_fusion
  471.9 2.8 multiply_divide_fusion.1
  (144 shorter events, 2.5 us)
Async XLA Ops:
  7.2 252.2 %reduce-scatter.2.cloned.1.call-start = ((), (), s32[]{:S(2)}) async-start(), calls=%async_computation.2 | async-start | bytes 20054016 | tf_op jit(solution)/shard_map/reduce_scatter | solution.py:68
  10.9 44.6 %copy-start = (bf16[512,2048]{1,0:T(8,128)(2,1)S(1)}, bf16[512,2048]{1,0:T(8,128)(2,1)}, u32[]{:S(2)}) copy-start(bf16[512,2048]{1,0:T(8,128)(2,1)} %param.8) | copy-start | bytes 6291460
  10.9 44.6 %copy-start.3 = (bf16[512,512]{1,0:T(8,128)(2,1)S(1)}, bf16[512,512]{1,0:T(8,128)(2,1)}, u32[]{:S(2)}) copy-start(bf16[512,512]{1,0:T(8,128)(2,1)} %param.10) | copy-start | bytes 1572868
  11.0 44.6 %copy-start.4 = (bf16[512,512]{1,0:T(8,128)(2,1)S(1)}, bf16[512,512]{1,0:T(8,128)(2,1)}, u32[]{:S(2)}) copy-start(bf16[512,512]{1,0:T(8,128)(2,1)} %param.9) | copy-start | bytes 1572868
  54.4 1.1 copy-start.1
  64.8 318.9 %all-gather.4.cloned.1.call-start = ((), (), s32[]{:S(2)}) async-start(), calls=%async_computation.3 | async-start | bytes 1671168 | tf_op jit(solution)/shard_map/all_gather | solution.py:103
  66.6 214.7 %collective-permute-start.17 = (bf16[256,512]{1,0:T(8,128)(2,1)}, bf16[256,512]{1,0:T(8,128)(2,1)}, u32[]{:S(2)}, u32[]{:S(2)}) collective-permute-start(bf16[256,512]{1,0:T(8,128)(2,1)} %get-tuple-element.21), channel_id=1, source_target_pairs={{0,1},{1,0},{2,3},{3,2},{4,5},{5,4},{6,7},{7,6},{8,9},{9,8},{10,11... | collective-permute-start | bytes 786440 | tf_op jit(solution)/shard_map/ppermute | solution.py:41
  69.7 218.3 %collective-permute-start.16 = (bf16[256,512]{1,0:T(8,128)(2,1)}, bf16[256,512]{1,0:T(8,128)(2,1)}, u32[]{:S(2)}, u32[]{:S(2)}) collective-permute-start(bf16[256,512]{1,0:T(8,128)(2,1)} %get-tuple-element.23), channel_id=1, source_target_pairs={{0,1},{1,0},{2,3},{3,2},{4,5},{5,4},{6,7},{7,6},{8,9},{9,8},{10,11... | collective-permute-start | bytes 786440 | tf_op jit(solution)/shard_map/ppermute | solution.py:41
  70.3 4.7 copy-start.34
  70.3 6.0 %copy-start.33 = (s32[96]{0:T(128)S(1)}, s32[96]{0:T(128)}, u32[]{:S(2)}) copy-start(s32[96]{0:T(128)} %param.11) | copy-start | bytes 1156
  73.5 221.3 %collective-permute-start.15 = (bf16[256,2048]{1,0:T(8,128)(2,1)}, bf16[256,2048]{1,0:T(8,128)(2,1)}, u32[]{:S(2)}, u32[]{:S(2)}) collective-permute-start(bf16[256,2048]{1,0:T(8,128)(2,1)} %get-tuple-element.17), channel_id=1, source_target_pairs={{0,1},{1,0},{2,3},{3,2},{4,5},{5,4},{6,7},{7,6},{8,9},{9,8},{10,11... | collective-permute-start | bytes 3145736 | tf_op jit(solution)/shard_map/ppermute | solution.py:41
  260.3 6.8 %collective-permute-start = (bf16[96,512]{1,0:T(8,128)(2,1)S(1)}, bf16[96,512]{1,0:T(8,128)(2,1)S(1)}, u32[]{:S(2)}, u32[]{:S(2)}) collective-permute-start(bf16[96,512]{1,0:T(8,128)(2,1)S(1)} %slice.46), channel_id=1, source_target_pairs={{0,2},{2,4},{4,6},{6,8},{8,10},{10,12},{12,14},{14,16},{16,18},{18... | collective-permute-start | bytes 294920 | tf_op jit(solution)/shard_map/ppermute | solution.py:107
  267.1 0.6 copy-start.7
  267.7 6.7 %collective-permute-start.1 = (bf16[96,512]{1,0:T(8,128)(2,1)S(1)}, bf16[96,512]{1,0:T(8,128)(2,1)S(1)}, u32[]{:S(2)}, u32[]{:S(2)}) collective-permute-start(bf16[96,512]{1,0:T(8,128)(2,1)S(1)} %collective-permute-done), channel_id=1, source_target_pairs={{0,2},{2,4},{4,6},{6,8},{8,10},{10,12},{12,14},{14,16},{16,18},{18... | collective-permute-start | bytes 294920 | tf_op jit(solution)/shard_map/ppermute | solution.py:107
  274.5 20.2 %copy-start.9 = (bf16[96,512]{1,0:T(8,128)(2,1)}, bf16[96,512]{1,0:T(8,128)(2,1)S(1)}, u32[]{:S(2)}) copy-start(bf16[96,512]{1,0:T(8,128)(2,1)S(1)} %collective-permute-done.1) | copy-start | bytes 294916
  274.5 6.7 %collective-permute-start.2 = (bf16[96,512]{1,0:T(8,128)(2,1)S(1)}, bf16[96,512]{1,0:T(8,128)(2,1)S(1)}, u32[]{:S(2)}, u32[]{:S(2)}) collective-permute-start(bf16[96,512]{1,0:T(8,128)(2,1)S(1)} %collective-permute-done.1), channel_id=1, source_target_pairs={{0,2},{2,4},{4,6},{6,8},{8,10},{10,12},{12,14},{14,16},{16,18},{18... | collective-permute-start | bytes 294920 | tf_op jit(solution)/shard_map/ppermute | solution.py:107
  279.5 22.0 %copy-start.2 = (bf16[96,16,512]{2,0,1:T(8,128)(2,1)S(1)}, bf16[96,16,512]{2,0,1:T(8,128)(2,1)}, u32[]{:S(2)}) copy-start(bf16[96,16,512]{2,0,1:T(8,128)(2,1)} %copy-done.1) | copy-start | bytes 4718596
  281.2 13.5 %copy-start.11 = (bf16[96,512]{1,0:T(8,128)(2,1)}, bf16[96,512]{1,0:T(8,128)(2,1)S(1)}, u32[]{:S(2)}) copy-start(bf16[96,512]{1,0:T(8,128)(2,1)S(1)} %collective-permute-done.2) | copy-start | bytes 294916
  281.2 6.7 %collective-permute-start.3 = (bf16[96,512]{1,0:T(8,128)(2,1)S(1)}, bf16[96,512]{1,0:T(8,128)(2,1)S(1)}, u32[]{:S(2)}, u32[]{:S(2)}) collective-permute-start(bf16[96,512]{1,0:T(8,128)(2,1)S(1)} %collective-permute-done.2), channel_id=1, source_target_pairs={{0,2},{2,4},{4,6},{6,8},{8,10},{10,12},{12,14},{14,16},{16,18},{18... | collective-permute-start | bytes 294920 | tf_op jit(solution)/shard_map/ppermute | solution.py:107
  288.0 6.8 %copy-start.13 = (bf16[96,512]{1,0:T(8,128)(2,1)}, bf16[96,512]{1,0:T(8,128)(2,1)S(1)}, u32[]{:S(2)}) copy-start(bf16[96,512]{1,0:T(8,128)(2,1)S(1)} %collective-permute-done.3) | copy-start | bytes 294916
  288.0 6.7 %collective-permute-start.4 = (bf16[96,512]{1,0:T(8,128)(2,1)S(1)}, bf16[96,512]{1,0:T(8,128)(2,1)S(1)}, u32[]{:S(2)}, u32[]{:S(2)}) collective-permute-start(bf16[96,512]{1,0:T(8,128)(2,1)S(1)} %collective-permute-done.3), channel_id=1, source_target_pairs={{0,2},{2,4},{4,6},{6,8},{8,10},{10,12},{12,14},{14,16},{16,18},{18... | collective-permute-start | bytes 294920 | tf_op jit(solution)/shard_map/ppermute | solution.py:107
  294.7 6.9 %copy-start.15 = (bf16[96,512]{1,0:T(8,128)(2,1)}, bf16[96,512]{1,0:T(8,128)(2,1)S(1)}, u32[]{:S(2)}) copy-start(bf16[96,512]{1,0:T(8,128)(2,1)S(1)} %collective-permute-done.4) | copy-start | bytes 294916
  294.7 6.7 %collective-permute-start.5 = (bf16[96,512]{1,0:T(8,128)(2,1)S(1)}, bf16[96,512]{1,0:T(8,128)(2,1)S(1)}, u32[]{:S(2)}, u32[]{:S(2)}) collective-permute-start(bf16[96,512]{1,0:T(8,128)(2,1)S(1)} %collective-permute-done.4), channel_id=1, source_target_pairs={{0,2},{2,4},{4,6},{6,8},{8,10},{10,12},{12,14},{14,16},{16,18},{18... | collective-permute-start | bytes 294920 | tf_op jit(solution)/shard_map/ppermute | solution.py:107
  294.7 35.0 %slice-start = ((f32[96,3072]{1,0:T(8,128)}), f32[96,512]{1,0:T(8,128)S(1)}, s32[]{:S(2)}) async-start(f32[96,3072]{1,0:T(8,128)} %reduce-scatter.2.cloned.1.call-done), calls=%async_computation.4 | async-start | bytes 393216 | tf_op jit(solution)/shard_map/slice | solution.py:72
  301.4 6.7 %copy-start.17 = (bf16[96,512]{1,0:T(8,128)(2,1)}, bf16[96,512]{1,0:T(8,128)(2,1)S(1)}, u32[]{:S(2)}) copy-start(bf16[96,512]{1,0:T(8,128)(2,1)S(1)} %collective-permute-done.5) | copy-start | bytes 294916
  301.5 6.7 %collective-permute-start.6 = (bf16[96,512]{1,0:T(8,128)(2,1)S(1)}, bf16[96,512]{1,0:T(8,128)(2,1)S(1)}, u32[]{:S(2)}, u32[]{:S(2)}) collective-permute-start(bf16[96,512]{1,0:T(8,128)(2,1)S(1)} %collective-permute-done.5), channel_id=1, source_target_pairs={{0,2},{2,4},{4,6},{6,8},{8,10},{10,12},{12,14},{14,16},{16,18},{18... | collective-permute-start | bytes 294920 | tf_op jit(solution)/shard_map/ppermute | solution.py:107
  308.2 0.6 copy-start.19
  308.2 6.7 %collective-permute-start.7 = (bf16[96,512]{1,0:T(8,128)(2,1)S(1)}, bf16[96,512]{1,0:T(8,128)(2,1)S(1)}, u32[]{:S(2)}, u32[]{:S(2)}) collective-permute-start(bf16[96,512]{1,0:T(8,128)(2,1)S(1)} %collective-permute-done.6), channel_id=1, source_target_pairs={{0,2},{2,4},{4,6},{6,8},{8,10},{10,12},{12,14},{14,16},{16,18},{18... | collective-permute-start | bytes 294920 | tf_op jit(solution)/shard_map/ppermute | solution.py:107
  314.9 14.8 %copy-start.21 = (bf16[96,512]{1,0:T(8,128)(2,1)}, bf16[96,512]{1,0:T(8,128)(2,1)S(1)}, u32[]{:S(2)}) copy-start(bf16[96,512]{1,0:T(8,128)(2,1)S(1)} %collective-permute-done.7) | copy-start | bytes 294916
  314.9 6.7 %collective-permute-start.8 = (bf16[96,512]{1,0:T(8,128)(2,1)S(1)}, bf16[96,512]{1,0:T(8,128)(2,1)S(1)}, u32[]{:S(2)}, u32[]{:S(2)}) collective-permute-start(bf16[96,512]{1,0:T(8,128)(2,1)S(1)} %collective-permute-done.7), channel_id=1, source_target_pairs={{0,2},{2,4},{4,6},{6,8},{8,10},{10,12},{12,14},{14,16},{16,18},{18... | collective-permute-start | bytes 294920 | tf_op jit(solution)/shard_map/ppermute | solution.py:107
  315.5 40.0 %copy-start.6 = (f32[96,64]{1,0:T(8,128)S(1)}, f32[96,64]{1,0:T(8,128)}, u32[]{:S(2)}) copy-start(f32[96,64]{1,0:T(8,128)} %get-tuple-element.30) | copy-start | bytes 73732
  321.7 8.1 %copy-start.23 = (bf16[96,512]{1,0:T(8,128)(2,1)}, bf16[96,512]{1,0:T(8,128)(2,1)S(1)}, u32[]{:S(2)}) copy-start(bf16[96,512]{1,0:T(8,128)(2,1)S(1)} %collective-permute-done.8) | copy-start | bytes 294916
  321.7 6.7 %collective-permute-start.9 = (bf16[96,512]{1,0:T(8,128)(2,1)S(1)}, bf16[96,512]{1,0:T(8,128)(2,1)S(1)}, u32[]{:S(2)}, u32[]{:S(2)}) collective-permute-start(bf16[96,512]{1,0:T(8,128)(2,1)S(1)} %collective-permute-done.8), channel_id=1, source_target_pairs={{0,2},{2,4},{4,6},{6,8},{8,10},{10,12},{12,14},{14,16},{16,18},{18... | collective-permute-start | bytes 294920 | tf_op jit(solution)/shard_map/ppermute | solution.py:107
  328.4 27.1 %copy-start.25 = (bf16[96,512]{1,0:T(8,128)(2,1)}, bf16[96,512]{1,0:T(8,128)(2,1)S(1)}, u32[]{:S(2)}) copy-start(bf16[96,512]{1,0:T(8,128)(2,1)S(1)} %collective-permute-done.9) | copy-start | bytes 294916
  328.4 6.7 %collective-permute-start.10 = (bf16[96,512]{1,0:T(8,128)(2,1)S(1)}, bf16[96,512]{1,0:T(8,128)(2,1)S(1)}, u32[]{:S(2)}, u32[]{:S(2)}) collective-permute-start(bf16[96,512]{1,0:T(8,128)(2,1)S(1)} %collective-permute-done.9), channel_id=1, source_target_pairs={{0,2},{2,4},{4,6},{6,8},{8,10},{10,12},{12,14},{14,16},{16,18},{18... | collective-permute-start | bytes 294920 | tf_op jit(solution)/shard_map/ppermute | solution.py:107
  335.2 20.3 %copy-start.27 = (bf16[96,512]{1,0:T(8,128)(2,1)}, bf16[96,512]{1,0:T(8,128)(2,1)S(1)}, u32[]{:S(2)}) copy-start(bf16[96,512]{1,0:T(8,128)(2,1)S(1)} %collective-permute-done.10) | copy-start | bytes 294916
  335.2 6.7 %collective-permute-start.11 = (bf16[96,512]{1,0:T(8,128)(2,1)S(1)}, bf16[96,512]{1,0:T(8,128)(2,1)S(1)}, u32[]{:S(2)}, u32[]{:S(2)}) collective-permute-start(bf16[96,512]{1,0:T(8,128)(2,1)S(1)} %collective-permute-done.10), channel_id=1, source_target_pairs={{0,2},{2,4},{4,6},{6,8},{8,10},{10,12},{12,14},{14,16},{16,18},{18... | collective-permute-start | bytes 294920 | tf_op jit(solution)/shard_map/ppermute | solution.py:107
  341.9 6.7 %collective-permute-start.12 = (bf16[96,512]{1,0:T(8,128)(2,1)S(1)}, bf16[96,512]{1,0:T(8,128)(2,1)S(1)}, u32[]{:S(2)}, u32[]{:S(2)}) collective-permute-start(bf16[96,512]{1,0:T(8,128)(2,1)S(1)} %collective-permute-done.11), channel_id=1, source_target_pairs={{0,2},{2,4},{4,6},{6,8},{8,10},{10,12},{12,14},{14,16},{16,18},{18... | collective-permute-start | bytes 294920 | tf_op jit(solution)/shard_map/ppermute | solution.py:107
  348.6 6.8 %collective-permute-start.13 = (bf16[96,512]{1,0:T(8,128)(2,1)S(1)}, bf16[96,512]{1,0:T(8,128)(2,1)S(1)}, u32[]{:S(2)}, u32[]{:S(2)}) collective-permute-start(bf16[96,512]{1,0:T(8,128)(2,1)S(1)} %collective-permute-done.12), channel_id=1, source_target_pairs={{0,2},{2,4},{4,6},{6,8},{8,10},{10,12},{12,14},{14,16},{16,18},{18... | collective-permute-start | bytes 294920 | tf_op jit(solution)/shard_map/ppermute | solution.py:107
  349.8 12.5 %copy-start.24 = (bf16[96,512]{1,0:T(8,128)(2,1)S(1)}, bf16[96,512]{1,0:T(8,128)(2,1)}, u32[]{:S(2)}) copy-start(bf16[96,512]{1,0:T(8,128)(2,1)} %copy-done.23) | copy-start | bytes 294916
  349.8 12.5 %copy-start.22 = (bf16[96,512]{1,0:T(8,128)(2,1)S(1)}, bf16[96,512]{1,0:T(8,128)(2,1)}, u32[]{:S(2)}) copy-start(bf16[96,512]{1,0:T(8,128)(2,1)} %copy-done.21) | copy-start | bytes 294916
  350.0 12.4 %copy-start.20 = (bf16[96,512]{1,0:T(8,128)(2,1)S(1)}, bf16[96,512]{1,0:T(8,128)(2,1)}, u32[]{:S(2)}) copy-start(bf16[96,512]{1,0:T(8,128)(2,1)} %copy-done.19) | copy-start | bytes 294916
  350.0 12.4 %copy-start.18 = (bf16[96,512]{1,0:T(8,128)(2,1)S(1)}, bf16[96,512]{1,0:T(8,128)(2,1)}, u32[]{:S(2)}) copy-start(bf16[96,512]{1,0:T(8,128)(2,1)} %copy-done.17) | copy-start | bytes 294916
  350.0 12.4 %copy-start.16 = (bf16[96,512]{1,0:T(8,128)(2,1)S(1)}, bf16[96,512]{1,0:T(8,128)(2,1)}, u32[]{:S(2)}) copy-start(bf16[96,512]{1,0:T(8,128)(2,1)} %copy-done.15) | copy-start | bytes 294916
  350.0 12.4 %copy-start.14 = (bf16[96,512]{1,0:T(8,128)(2,1)S(1)}, bf16[96,512]{1,0:T(8,128)(2,1)}, u32[]{:S(2)}) copy-start(bf16[96,512]{1,0:T(8,128)(2,1)} %copy-done.13) | copy-start | bytes 294916
  355.5 6.7 %collective-permute-start.14 = (bf16[96,512]{1,0:T(8,128)(2,1)S(1)}, bf16[96,512]{1,0:T(8,128)(2,1)S(1)}, u32[]{:S(2)}, u32[]{:S(2)}) collective-permute-start(bf16[96,512]{1,0:T(8,128)(2,1)S(1)} %collective-permute-done.13), channel_id=1, source_target_pairs={{0,2},{2,4},{4,6},{6,8},{8,10},{10,12},{12,14},{14,16},{16,18},{18... | collective-permute-start | bytes 294920 | tf_op jit(solution)/shard_map/ppermute | solution.py:107
  355.5 6.8 %copy-start.28 = (bf16[96,512]{1,0:T(8,128)(2,1)S(1)}, bf16[96,512]{1,0:T(8,128)(2,1)}, u32[]{:S(2)}) copy-start(bf16[96,512]{1,0:T(8,128)(2,1)} %copy-done.27) | copy-start | bytes 294916
  355.5 6.8 %copy-start.26 = (bf16[96,512]{1,0:T(8,128)(2,1)S(1)}, bf16[96,512]{1,0:T(8,128)(2,1)}, u32[]{:S(2)}) copy-start(bf16[96,512]{1,0:T(8,128)(2,1)} %copy-done.25) | copy-start | bytes 294916
  355.5 7.0 %copy-start.12 = (bf16[96,512]{1,0:T(8,128)(2,1)S(1)}, bf16[96,512]{1,0:T(8,128)(2,1)}, u32[]{:S(2)}) copy-start(bf16[96,512]{1,0:T(8,128)(2,1)} %copy-done.11) | copy-start | bytes 294916
  355.5 7.0 %copy-start.10 = (bf16[96,512]{1,0:T(8,128)(2,1)S(1)}, bf16[96,512]{1,0:T(8,128)(2,1)}, u32[]{:S(2)}) copy-start(bf16[96,512]{1,0:T(8,128)(2,1)} %copy-done.9) | copy-start | bytes 294916
  355.5 7.0 %copy-start.8 = (bf16[96,512]{1,0:T(8,128)(2,1)S(1)}, bf16[96,512]{1,0:T(8,128)(2,1)}, u32[]{:S(2)}) copy-start(bf16[96,512]{1,0:T(8,128)(2,1)} %copy-done.7) | copy-start | bytes 294916
  355.5 7.0 %copy-start.5 = (f32[96,3072]{1,0:T(8,128)S(1)}, f32[96,3072]{1,0:T(8,128)}, u32[]{:S(2)}) copy-start(f32[96,3072]{1,0:T(8,128)} %reduce-scatter.2.cloned.1.call-done) | copy-start | bytes 3538948
  391.3 2.6 copy-start.30
  453.3 18.6 %copy-start.31 = (f32[512]{0:T(512)}, f32[512]{0:T(512)S(1)}, u32[]{:S(2)}) copy-start(f32[512]{0:T(512)S(1)} %maximum_multiply_fusion.2) | copy-start | bytes 6148
  457.6 14.3 %copy-start.32 = (f32[512]{0:T(512)}, f32[512]{0:T(512)S(1)}, u32[]{:S(2)}) copy-start(f32[512]{0:T(512)S(1)} %maximum_multiply_fusion.1) | copy-start | bytes 6148
  462.0 9.9 %copy-start.29 = (f32[2048]{0:T(1024)}, f32[2048]{0:T(1024)S(1)}, u32[]{:S(2)}) copy-start(f32[2048]{0:T(1024)S(1)} %maximum_multiply_fusion) | copy-start | bytes 24580
Sparse Core Ops, SparseCore 0:
  64.9 194.4 reduce-scatter.1
  342.8 40.7 all-gather.3
